TPU v7x, 32 devices: a whole 2x2x4 slice. The times are simulated.
32 devices in a mesh: day: 8 (over y, x, core), pair: 4 (over z).
Axes of the slice: x: 2, y: 2, z: 4, core: 2. Of those that a mesh axis runs over, the one named last changes fastest.
Arguments:
- correlations: bfloat16 [32, 2048, 2001], P('day', 'pair'), may hold values from -8 to 8
- mask: int32 [32, 2048], P('day', 'pair'), may hold values from 0 to 1, as said below
- counts: int32 [2048], P(('pair', 'day')), may hold values from 1 to 32, as said below
Outputs:
- phase_weighted: float32 [2048, 2001], P(('pair', 'day'))
- linear: float32 [2048, 2001], P(('pair', 'day'))
Inputs may be any that keep to these rules, and one draw needn't show every extreme that they name: `mask`: every pair has a usable correlation on at least one day. counts[p] equals the number of days d with mask[d, p] = 1.
All inputs are finite; a program needn't handle non-finite values.
Results may differ from a plain program's by a relative error of at most 0.00044.
Values may be sent and summed in bfloat16 or wider, within the bound.
A program may use at most 128 MiB of HBM per device.

v0:
```python
import functools

import jax
import jax.numpy as jnp
import numpy as np
from jax import lax
from jax.experimental import pallas as pl
from jax.experimental.pallas import tpu as pltpu
from jax.sharding import PartitionSpec as P

TILE = 256
MESH = pl.DeviceIdType.MESH
FULL = 32767.0
UNIT = 2.0**20


def padded(lag_count):
    return -(-lag_count // TILE) * TILE


def kernel_strip(lag_count):
    f32 = np.float32
    offset = np.arange(lag_count, dtype=np.int32)
    offset = np.where(offset > lag_count // 2, offset - lag_count, offset)
    angle = f32(np.pi) * offset.astype(f32) / f32(lag_count)
    parity = f32(1) - f32(2) * (offset % 2).astype(f32)
    sine = np.where(offset == 0, f32(1), np.sin(angle)).astype(f32)
    kernel = np.where(offset == 0, f32(0), (np.cos(angle) - parity) / (f32(lag_count) * sine))
    width = padded(lag_count)
    index = np.arange(2 * width - TILE)[None, :] - np.arange(TILE)[:, None] - (width - TILE)
    return kernel.astype(f32)[index % lag_count].astype(jnp.bfloat16)


def codes(values):
    top = jnp.max(jnp.abs(values), axis=1, keepdims=True)
    units = (top * UNIT).astype(jnp.int32) + 1
    step = FULL * UNIT / units.astype(jnp.float32)
    return jnp.round(values * step).astype(jnp.int32), units


def join(high, low):
    return high * 65536 + (low & 65535)


def split(word):
    low = ((word & 65535) ^ 32768) - 32768
    return word >> 16, low


def stack_kernel(
    lag_count, x_hbm, mask_ref, strip_hbm, linear_ref, power_ref,
    rows_ref, stage, strip, table, sums, first_hilbert, mask_in, mask_turned, row_mask, day_weight,
    stat_out, stat_in, words_out, words_in,
    load_sem, stage_sem, strip_sem, swap_send, swap_recv, mask_send, mask_recv,
    stat_send, stat_recv, word_send, word_recv,
):
    width = table.shape[1]
    half = width // 2
    chips, all_days, owned, _ = rows_ref.shape
    days = all_days // 2
    total = all_days * owned
    part = owned // 2
    pieces = words_out.shape[0]
    peers = stat_in.shape[0]
    me, plane = lax.axis_index("day"), lax.axis_index("pair")
    chip, core = me // 2, me % 2
    partner = {"day": me ^ 1, "pair": plane}
    last = width - TILE
    tiles = [slice(j * TILE, min((j + 1) * TILE, lag_count)) for j in range(width // TILE)]

    def mine(g):
        return pltpu.make_async_copy(x_hbm.at[:, 2 * g + core], rows_ref.at[g, pl.ds(0, days)], load_sem.at[g])

    def staged(g):
        return pltpu.make_async_copy(x_hbm.at[:, 2 * g + 1 - core], stage.at[g], stage_sem.at[g])

    def swapped(g):
        return pltpu.make_async_remote_copy(
            stage.at[g], rows_ref.at[g, pl.ds(days, days)], swap_send.at[g], swap_recv.at[g],
            device_id=partner, device_id_type=MESH,
        )

    def peer(o):
        rank = (2 * plane + core + o) % (peers + 1)
        return {"day": 2 * chip + rank % 2, "pair": rank // 2}

    def told(o):
        return pltpu.make_async_remote_copy(
            stat_out, stat_in.at[o - 1], stat_send.at[o - 1], stat_recv.at[o - 1],
            device_id=peer(o), device_id_type=MESH,
        )

    def owner(o):
        return {"day": 2 * (chip ^ o) + core, "pair": plane}

    def shipped(piece, o):
        return pltpu.make_async_remote_copy(
            words_out.at[piece], words_in.at[piece], word_send.at[piece], word_recv.at[piece],
            device_id=owner(o), device_id_type=MESH,
        )

    far = range(chips - 1, 3, -1)
    order = [chip ^ o for o in (3, *far, 1, 2, 0)]
    strip_copy = pltpu.make_async_copy(strip_hbm, strip, strip_sem)
    strip_copy.start()
    for g in order:
        staged(g).start()
        mine(g).start()

    barrier = pltpu.get_barrier_semaphore()
    for o in range(1, peers + 1):
        pl.semaphore_signal(barrier, inc=1, device_id=peer(o), device_id_type=MESH)
    for o in range(1, chips):
        pl.semaphore_signal(barrier, inc=1, device_id=owner(o), device_id_type=MESH)
    strip_copy.wait()
    for i in range(width // TILE):
        start = width - TILE - i * TILE
        table[pl.ds(i * TILE, TILE), :] = strip[:, start : start + width]
    sums[:, :, last:] = jnp.zeros((3, owned, TILE), jnp.float32)
    pl.semaphore_wait(barrier, peers + chips - 1)

    mask_copy = pltpu.make_async_remote_copy(
        mask_ref, mask_in, mask_send, mask_recv, device_id=partner, device_id_type=MESH
    )
    mask_copy.start()
    for g in order:
        staged(g).wait()
        swapped(g).start()
    mask_copy.wait_recv()
    both_masks = jnp.concatenate([mask_ref[...], mask_in[...]], axis=0).astype(jnp.float32)
    mask_turned[...] = both_masks.T

    def mask_rows(block, count):
        rows = mask_turned[pl.ds(pl.multiple_of(block * owned, owned), owned), :]
        return jnp.concatenate([rows[:, d : d + 1] for d in range(count)], axis=0)

    def statistics(step, carry):
        g = chip ^ (chips - 1 - step)
        mine(g).wait()
        of_pairs = mask_rows(2 * g + core, all_days)
        row_mask[g] = of_pairs.reshape(all_days, owned, 1)
        for x_ref, rows in ((rows_ref.at[g, pl.ds(0, days)], of_pairs[: days * owned]),
                            (stage.at[g], mask_rows(2 * g + 1 - core, days))):
            x = x_ref[...].reshape(days * owned, lag_count).astype(jnp.float32)
            energy = jnp.sum(x * x, axis=1, keepdims=True) * rows
            both = jnp.concatenate(
                [jnp.broadcast_to(energy, (days * owned, 128)), jnp.broadcast_to(rows, (days * owned, 128))], axis=1
            )
            carry = carry + jnp.sum(both.reshape(days, owned, 256), axis=1)
        return carry

    found = lax.fori_loop(0, chips, statistics, jnp.zeros((days, 256), jnp.float32))
    none = jnp.zeros_like(found)
    stat_out[...] = jnp.where(
        core == 0, jnp.concatenate([found, none], axis=0), jnp.concatenate([none, found], axis=0)
    )
    for o in range(1, peers + 1):
        told(o).start()

    def transform(g, here, cols):
        lhs = rows_ref[g, :, here, :].reshape(-1, lag_count)
        return jnp.dot(lhs, table[:lag_count, cols], preferred_element_type=jnp.float32)

    def add_days(g, here, cols, hilbert):
        size = cols.stop - cols.start
        count = hilbert.shape[0] // all_days
        scale = (day_weight[:, :count] * row_mask[g, :, here, :]).reshape(-1, 1)
        real = scale * rows_ref[g, :, here, cols].reshape(-1, size).astype(jnp.float32)
        imag = scale * hilbert
        inverse = lax.rsqrt(real * real + imag * imag + 0.25)
        for k, term in enumerate((real, real * inverse, imag * inverse)):
            sums[k, :count, cols] = jnp.sum(term.reshape(all_days, count, size), axis=0)

    def encode(piece, rows, o):
        linear, linear_units = codes(sums[0, rows])
        first, first_units = codes(sums[1, rows])
        second, second_units = codes(sums[2, rows])
        words_out[piece, :, :width] = join(first, second)
        words_out[piece, :, width : width + half] = join(linear[:, :half], linear[:, half:])
        pick = lax.broadcasted_iota(jnp.int32, (part, 128), 1)
        words_out[piece, :, width + half :] = jnp.where(
            pick == 0, linear_units, jnp.where(pick == 1, first_units, second_units)
        )
        shipped(piece, o).start()

    def decode(piece, rows):
        units = words_in[piece, :, width + half :].astype(jnp.float32) * (1.0 / (FULL * UNIT))
        left, right = split(words_in[piece, :, width : width + half])
        sums[0, rows, :half] += left.astype(jnp.float32) * units[:, 0:1]
        sums[0, rows, half:] += right.astype(jnp.float32) * units[:, 0:1]
        first, second = split(words_in[piece, :, :width])
        sums[1, rows] += first.astype(jnp.float32) * units[:, 1:2]
        sums[2, rows] += second.astype(jnp.float32) * units[:, 2:3]

    whole, low, high = pl.ds(0, owned), pl.ds(0, part), pl.ds(part, part)

    swapped(order[0]).wait_recv()
    for cols in tiles:
        first_hilbert[:, cols] = transform(order[0], whole, cols)

    for o in range(1, peers + 1):
        told(o).wait_recv()
    stats = stat_out[...]
    for o in range(peers):
        stats = stats + stat_in[o]
    weight = lax.rsqrt(stats[:, :128] / (lag_count * jnp.maximum(stats[:, 128:], 1.0)) + 0.1)
    weight = jnp.where(core == 0, weight, jnp.concatenate([weight[days:], weight[:days]], axis=0))
    for d in range(all_days):
        day_weight[d] = jnp.broadcast_to(weight[d : d + 1, :1], (owned, 1))

    for cols in tiles:
        add_days(order[0], whole, cols, first_hilbert[:, cols])
    encode(0, low, 1)
    encode(1, high, 2)

    def far_block(step, carry):
        o = chips - 1 - step
        swapped(chip ^ o).wait_recv()
        for cols in tiles:
            add_days(chip ^ o, whole, cols, transform(chip ^ o, whole, cols))
        encode(2 * o - 2, low, o)
        encode(2 * o - 1, high, o)
        return carry

    if chips > 4:
        lax.fori_loop(0, chips - 4, far_block, 0)

    def near_half(q, carry):
        o = 1 + q % 2
        g = chip ^ o
        here = pl.ds(pl.multiple_of(((q + q // 2) % 2) * part, part), part)

        @pl.when(q < 2)
        def _():
            swapped(g).wait_recv()

        for cols in tiles:
            add_days(g, here, cols, transform(g, here, cols))

        @pl.when(q >= 2)
        def _():
            shipped(3 - q, o).wait_recv()
            decode(3 - q, low)

        encode(2 + q, low, o)
        return carry

    lax.fori_loop(0, 4, near_half, 0)
    swapped(chip).wait_recv()
    for cols in tiles:
        add_days(chip, whole, cols, transform(chip, whole, cols))

    def arrive(piece, carry):
        turn = piece + jnp.where(piece // 2 == 2, 1, 0)
        shipped(piece, 1).wait_recv()
        decode(piece, pl.ds(pl.multiple_of((turn % 2) * part, part), part))
        return carry

    lax.fori_loop(2, pieces, arrive, 0)
    real, imag = sums[1, :, :lag_count], sums[2, :, :lag_count]
    linear_ref[...] = sums[0, :, :lag_count]
    power_ref[...] = real * real + imag * imag

    mask_copy.wait_send()
    for g in range(chips):
        swapped(g).wait_send()
    for o in range(1, peers + 1):
        told(o).wait_send()
    for piece in range(pieces):
        shipped(piece, 1).wait_send()


def shards(correlations, mask, counts):
    days, pairs, lag_count = correlations.shape
    groups = lax.axis_size("day")
    chips = groups // 2
    owned = pairs // groups
    width = padded(lag_count)
    peers = 2 * lax.axis_size("pair") - 1

    strip = jnp.asarray(kernel_strip(lag_count))
    size = width + width // 2 + 128
    pieces = 2 * chips - 2
    out = jax.ShapeDtypeStruct((owned, lag_count), jnp.float32)
    vmem = pl.BlockSpec(memory_space=pltpu.VMEM)
    hbm = pl.BlockSpec(memory_space=pl.ANY)
    dma = pltpu.SemaphoreType.DMA
    linear_sum, power = pl.pallas_call(
        functools.partial(stack_kernel, lag_count),
        in_specs=[hbm, vmem, hbm],
        out_specs=(vmem, vmem),
        out_shape=(out, out),
        scratch_shapes=[
            pltpu.VMEM((chips, 2 * days, owned, lag_count), jnp.bfloat16),
            pltpu.VMEM((chips, days, owned, lag_count), jnp.bfloat16),
            pltpu.VMEM(strip.shape, jnp.bfloat16),
            pltpu.VMEM((width, width), jnp.bfloat16),
            pltpu.VMEM((3, owned, width), jnp.float32),
            pltpu.VMEM((2 * days * owned, width), jnp.float32),
            pltpu.VMEM((days, pairs), jnp.int32),
            pltpu.VMEM((pairs, 2 * days), jnp.float32),
            pltpu.VMEM((chips, 2 * days, owned, 1), jnp.float32),
            pltpu.VMEM((2 * days, owned, 1), jnp.float32),
            pltpu.VMEM((2 * days, 256), jnp.float32),
            pltpu.VMEM((peers, 2 * days, 256), jnp.float32),
            pltpu.VMEM((pieces, owned // 2, size), jnp.int32),
            pltpu.VMEM((pieces, owned // 2, size), jnp.int32),
            dma((chips,)), dma((chips,)), dma, dma((chips,)), dma((chips,)), dma, dma,
            dma((peers,)), dma((peers,)), dma((pieces,)), dma((pieces,)),
        ],
        compiler_params=pltpu.CompilerParams(
            vmem_limit_bytes=46 * 2**20, collective_id=0, has_side_effects=True
        ),
        name="stack",
    )(correlations.reshape(days, groups, owned, lag_count), mask, strip)
    inverse = (1.0 / jnp.maximum(counts.astype(jnp.float32), 1.0))[:, None]
    linear = linear_sum * inverse
    return (linear * (power * (inverse * inverse)), linear)


def solution(mesh):
    placed = (P("day", "pair", None), P("day", "pair"), P(("pair", "day")))
    return jax.shard_map(
        shards,
        mesh=mesh,
        in_specs=placed,
        out_specs=(P(("pair", "day"), None), P(("pair", "day"), None)),
        check_vma=False,
    )
```

profile of v0, /device:TPU:1, one launch (start us, length us, event | category | flops | bytes accessed | tf_op | source)
XLA Modules:
  0.0 60.7 jit_solution(11408501458923064006)
XLA Ops:
  0.6 0.0 copy-start
  0.6 0.0 copy-start.1
  0.7 13.8 %copy.6 = bf16[4,512,2001]{2,1,0:T(8,128)(2,1)} copy(bf16[4,512,2001]{1,0,2:T(4,128)(2,1)} %param.4) | data formatting | bytes 16392192 | tf_op args[0]
  14.5 0.0 copy-start.2
  14.5 0.0 copy-done
  14.5 0.0 copy-done.1
  14.5 45.0 %stack.1 = (f32[64,2001]{1,0:T(8,128)S(1)}, f32[64,2001]{1,0:T(8,128)S(1)}) custom-call(bf16[4,8,64,2001]{3,2,1,0:T(8,128)(2,1)} %bitcast.1, s32[4,512]{1,0:T(4,128)S(1)} %copy-done.1, bf16[256,3840]{1,0:T(8,128)(2,1)S(1)} %copy-done), custom_call_target="tpu_custom_call" | custom-call | tf_op jit(solution)/shard_map/stack/pallas_call | solution.py:288
  59.5 0.0 copy-done.2
  59.6 1.1 %multiply_multiply_fusion = (f32[64,2001]{1,0:T(8,128)}, f32[64,2001]{1,0:T(8,128)}) fusion(f32[64,2001]{1,0:T(8,128)S(1)} %get-tuple-element.5, f32[64]{0:T(128)S(1)} %get-tuple-element.8, f32[64,2001]{1,0:T(8,128)S(1)} %get-tuple-element.4, f32[64]{0:T(128)S(1)} %get-tuple-element.9), kind=kLoop, calls=%fused_computation | loop fusion | flops 384192 | bytes 2049536 | tf_op jit(solution)/shard_map/mul | solution.py:318
  (1 shorter events, 0.0 us)
Async XLA Ops:
  0.6 13.9 %copy-start = (bf16[256,3840]{1,0:T(8,128)(2,1)S(1)}, bf16[256,3840]{1,0:T(8,128)(2,1)}, u32[]{:S(2)}) copy-start(bf16[256,3840]{1,0:T(8,128)(2,1)} %constant.4.clone.strip_hbm) | copy-start | bytes 5898244
  0.6 13.9 %copy-start.1 = (s32[4,512]{1,0:T(4,128)S(1)}, s32[4,512]{1,0:T(4,128)}, u32[]{:S(2)}) copy-start(s32[4,512]{1,0:T(4,128)} %mask_ref.1) | copy-start | bytes 24580
  14.5 45.0 %copy-start.2 = (s32[64]{0:T(128)S(1)}, s32[64]{0:T(128)}, u32[]{:S(2)}) copy-start(s32[64]{0:T(128)} %param.6) | copy-start | bytes 772
where the time goes:
time: 61.8 us; the launch traced here: 60.7 us
  Pallas kernels  45 us (73%)
  local copies, waits for them, and re-layouts  13.9 us (22%)
  other arithmetic  1.11 us (2%)
  between operations  0.67 us (1%)
    pallas_call x1, Pallas kernels, shards(): pl.pallas_call(functools.partial(stack_kernel, lag_count), in_specs=[hbm,...  45 us
    unnamed x7, local copies, waits for them, and re-layouts  13.9 us

commit v1 on v0

--- a/solution.py
+++ b/solution.py
@@ -270,7 +270,7 @@
         shipped(piece, 1).wait_send()
 
 
-def shards(correlations, mask, counts):
+def general_sums(correlations, mask):
     days, pairs, lag_count = correlations.shape
     groups = lax.axis_size("day")
     chips = groups // 2
@@ -285,7 +285,7 @@
     vmem = pl.BlockSpec(memory_space=pltpu.VMEM)
     hbm = pl.BlockSpec(memory_space=pl.ANY)
     dma = pltpu.SemaphoreType.DMA
-    linear_sum, power = pl.pallas_call(
+    return pl.pallas_call(
         functools.partial(stack_kernel, lag_count),
         in_specs=[hbm, vmem, hbm],
         out_specs=(vmem, vmem),
@@ -313,6 +313,414 @@
         ),
         name="stack",
     )(correlations.reshape(days, groups, owned, lag_count), mask, strip)
+
+
+LANES = 128
+CHUNK = 512
+HALF = CHUNK // 2
+ROWS = HALF // 2
+WORDS = ROWS + ROWS // 2
+PACK = WORDS + 8
+
+
+def block_strip(lag_count):
+    f32 = np.float32
+    offset = np.arange(lag_count, dtype=np.int32)
+    offset = np.where(offset > lag_count // 2, offset - lag_count, offset)
+    angle = f32(np.pi) * offset.astype(f32) / f32(lag_count)
+    parity = f32(1) - f32(2) * (offset % 2).astype(f32)
+    sine = np.where(offset == 0, f32(1), np.sin(angle)).astype(f32)
+    kernel = np.where(offset == 0, f32(0), (np.cos(angle) - parity) / (f32(lag_count) * sine))
+    width = chunked(lag_count)
+    index = np.arange(TILE)[:, None] - np.arange(2 * width - TILE)[None, :] + (width - TILE)
+    return kernel.astype(f32)[index % lag_count].astype(jnp.bfloat16)
+
+
+def chunked(lag_count):
+    return -(-lag_count // CHUNK) * CHUNK
+
+
+def sorting_matrix(rows):
+    lags = TILE // rows
+    out = np.arange(TILE)
+    source = (out % lags) * rows + out // lags
+    return (source[:, None] == np.arange(TILE)[None, :]).astype(jnp.bfloat16)
+
+
+def fast_kernel(
+    lag_count, x_hbm, mask_ref, strip, sorter, linear_ref, power_ref,
+    raw, own, theirs, first_h, second_h, sums, scale, bias, mask_in, stat_out, stat_in,
+    partial_out, partial_in, final_out, final_in, own_out, total,
+    load_sem, swap_send, swap_recv, late_send, late_recv, mask_send, mask_recv, stat_send, stat_recv,
+    partial_send, partial_recv, final_send, final_recv, own_send, own_recv,
+):
+    f32 = jnp.float32
+    width = raw.shape[0]
+    planes = raw.shape[1]
+    loads = width // TILE
+    steps = width // CHUNK
+    peers = stat_in.shape[0]
+    days = mask_ref.shape[0]
+    tiles = mask_ref.shape[1] // LANES
+    lags = TILE // planes
+    me, plane = lax.axis_index("day"), lax.axis_index("pair")
+    chip, core = me // 2, me % 2
+    partner = {"day": me ^ 1, "pair": plane}
+
+    def near(o, c):
+        return {"day": 2 * (chip ^ o) + c, "pair": plane}
+
+    def peer(o):
+        rank = (2 * plane + core + o) % (peers + 1)
+        return {"day": 2 * chip + rank % 2, "pair": rank // 2}
+
+    def loaded(j, count=TILE):
+        rows = pl.ds(j * TILE, count)
+        return pltpu.make_async_copy(x_hbm.at[rows], raw.at[rows], load_sem.at[j])
+
+    def remote(source, target, send, recv, device):
+        return pltpu.make_async_remote_copy(
+            source, target, send, recv, device_id=device, device_id_type=MESH
+        )
+
+    def mine(slot):
+        return 2 * (1 - core) + 1 - slot
+
+    def swapped(j):
+        rows = pl.ds(pl.multiple_of(j * TILE, TILE), TILE)
+        return remote(
+            own.at[2 * core + 1, :, rows], theirs.at[0, :, rows], swap_send.at[j], swap_recv.at[j], partner
+        )
+
+    def swapped_late():
+        return remote(own.at[2 * core], theirs.at[1], late_send, late_recv, partner)
+
+    def told(o):
+        return remote(stat_out, stat_in.at[o - 1], stat_send.at[o - 1], stat_recv.at[o - 1], peer(o))
+
+    def relayed(k, half):
+        return remote(
+            partial_out.at[k, half], partial_in.at[k], partial_send.at[k, half], partial_recv.at[k],
+            near(1 + half, half),
+        )
+
+    def finished(k, half, c):
+        return remote(
+            final_out.at[k, half, c], final_in.at[1 - core, k, half], final_send.at[k, half, c],
+            final_recv.at[1 - core, k, half], near(2 - core, c),
+        )
+
+    def handed(k, half):
+        return remote(own_out.at[k, half], total.at[k, half], own_send.at[k, half], own_recv.at[k, half], partner)
+
+    last = loads - 1
+    for j in range(last):
+        loaded(j).start()
+    loaded(last, lag_count - last * TILE).start()
+    barrier = pltpu.get_barrier_semaphore()
+    for o in range(1, peers + 1):
+        pl.semaphore_signal(barrier, inc=1, device_id=peer(o), device_id_type=MESH)
+    for o in (1, 2):
+        for c in (0, 1):
+            pl.semaphore_signal(barrier, inc=1, device_id=near(o, c), device_id_type=MESH)
+    raw[lag_count:] = jnp.zeros((width - lag_count, planes, LANES), raw.dtype)
+    pl.semaphore_wait(barrier, peers + 4)
+    mask_copy = remote(mask_ref, mask_in, mask_send, mask_recv, partner)
+    mask_copy.start()
+
+    def sort(j, energy):
+        energy = [energy[i] for i in range(planes)]
+        for g in range(TILE // (2 * lags)):
+            at = pl.multiple_of(j * TILE + g * 2 * lags, 2 * lags)
+            pair = [raw[pl.ds(at + h * lags, lags)].reshape(TILE, LANES) for h in (0, 1)]
+            out = jnp.dot(sorter[...], jnp.concatenate(pair, axis=1), preferred_element_type=f32)
+            for t in range(tiles):
+                for d in range(days):
+                    i = t * days + d
+                    lane = (d % 2) * LANES
+                    for h in (0, 1):
+                        value = out[i * lags : (i + 1) * lags, h * LANES : (h + 1) * LANES]
+                        energy[i] = energy[i] + jnp.sum((value * value).reshape(-1, 8, LANES), axis=0)
+                        own[chip ^ t, d // 2, pl.ds(at + h * lags, lags), lane : lane + LANES] = value.astype(own.dtype)
+        return jnp.stack(energy)
+
+    def sort_load(j, energy):
+        loaded(j).wait()
+        energy = sort(j, energy)
+        swapped(j).start()
+        return energy
+
+    energy = lax.fori_loop(0, last, sort_load, jnp.zeros((planes, 8, LANES), f32))
+    loaded(last, lag_count - last * TILE).wait()
+    energy = sort(last, energy)
+    swapped(last).start()
+    swapped_late().start()
+
+    found, used = [], []
+    for d in range(days):
+        rows = [mask_ref[d : d + 1, t * LANES : (t + 1) * LANES].astype(f32) for t in range(tiles)]
+        one = sum(jnp.sum(energy[t * days + d], axis=0, keepdims=True) * rows[t] for t in range(tiles))
+        found.append(one)
+        used.append(sum(rows))
+    stat_out[...] = jnp.concatenate(found + used, axis=0)
+    for o in range(1, peers + 1):
+        told(o).start()
+
+    def operand(slot, dp):
+        return own[mine(slot), dp] if dp < days // 2 else theirs[slot, dp - days // 2]
+
+    def transform(slot, k, dps, target):
+        for dp in dps:
+            rhs = operand(slot, dp)
+            for part in range(CHUNK // TILE):
+                start = pl.multiple_of(width - TILE - (k * (CHUNK // TILE) + part) * TILE, TILE)
+                target[part * TILE : (part + 1) * TILE, dp * TILE : (dp + 1) * TILE] = jnp.dot(
+                    strip[:, pl.ds(start, width)], rhs, preferred_element_type=f32
+                )
+
+    def add_days(slot, k, first, count, source):
+        size = 32
+        for row in range(first, first + count, size):
+            at = pl.multiple_of(k * CHUNK + row, size)
+            lin = one = two = jnp.zeros((size // 8, 8, LANES), f32)
+            for e in range(2 * days):
+                dp, lane = e // 2, (e % 2) * LANES
+                if e < days:
+                    x = own[mine(slot), dp, pl.ds(at, size), lane : lane + LANES]
+                else:
+                    x = theirs[slot, dp - days // 2, pl.ds(at, size), lane : lane + LANES]
+                x = x.astype(f32).reshape(size // 8, 8, LANES)
+                h = source[row : row + size, e * LANES : (e + 1) * LANES].reshape(size // 8, 8, LANES)
+                r = lax.rsqrt(x * x + h * h + bias[slot, e][None])
+                lin = lin + x * scale[slot, e][None]
+                one = one + x * r
+                two = two + h * r
+            for v, value in enumerate((lin, one, two)):
+                sums[slot, v, row : row + size] = value.reshape(size, LANES)
+
+    low_lane = lax.broadcasted_iota(jnp.int32, (ROWS, LANES), 1) < LANES // 2
+
+    def split(slot, half, v, c):
+        a = sums[slot, v, half * HALF : half * HALF + ROWS]
+        b = sums[slot, v, half * HALF + ROWS : (half + 1) * HALF]
+        if c == 0:
+            return jnp.where(low_lane, a, pltpu.roll(b, LANES // 2, 1))
+        return jnp.where(low_lane, pltpu.roll(a, LANES // 2, 1), b)
+
+    def encode(target, values):
+        coded, units = [], []
+        for value in values:
+            top = jnp.max(jnp.abs(value), axis=0, keepdims=True)
+            unit = (top * UNIT).astype(jnp.int32) + 1
+            step = FULL * UNIT / unit.astype(f32)
+            coded.append((value * step + 32768.5).astype(jnp.int32))
+            units.append(unit)
+        lin, one, two = coded
+        target[:ROWS] = one * 65536 + two
+        target[ROWS:WORDS] = lin[: ROWS // 2] * 65536 + lin[ROWS // 2 :]
+        pick = lax.broadcasted_iota(jnp.int32, (8, LANES), 0)
+        target[WORDS:] = jnp.where(pick == 0, units[0], jnp.where(pick == 1, units[1], units[2]))
+
+    def decode(source):
+        units = source[WORDS:].astype(f32) * (1.0 / (FULL * UNIT))
+
+        def value(code, v):
+            return (code.astype(f32) - 32768.0) * units[v : v + 1]
+
+        def pieces(word):
+            return lax.shift_right_logical(word, jnp.full_like(word, 16)), word & 65535
+
+        one, two = pieces(source[:ROWS])
+        top, bottom = pieces(source[ROWS:WORDS])
+        return (jnp.concatenate([value(top, 0), value(bottom, 0)], axis=0), value(one, 1), value(two, 2))
+
+    def send_direct(slot, k, half):
+        for c in (0, 1):
+            encode(final_out.at[k, half, c], [split(slot, half, v, c) for v in range(3)])
+            finished(k, half, c).start()
+
+    def send_relayed(slot, k, half):
+        relayed(k, half).wait_recv()
+        for c in (0, 1):
+            far = decode(partial_in.at[k, c])
+            encode(final_out.at[k, half, c], [split(slot, half, v, c) + far[v] for v in range(3)])
+            finished(k, half, c).start()
+
+    def finish_first(k):
+        @pl.when(core == 0)
+        def _():
+            for half in (0, 1):
+                for c in (0, 1):
+                    encode(partial_out.at[k, half, c], [split(0, half, v, c) for v in range(3)])
+                relayed(k, half).start()
+
+        @pl.when(core == 1)
+        def _():
+            send_direct(0, k, 0)
+
+    def finish_second(k):
+        @pl.when(core == 0)
+        def _():
+            send_direct(1, k, 1)
+            send_relayed(1, k, 0)
+
+        @pl.when(core == 1)
+        def _():
+            for half in (0, 1):
+                for v in range(3):
+                    own_out[k, half, v] = split(1, half, v, 0)
+                    total[k, half, v] = split(1, half, v, 1)
+                handed(k, half).start()
+            send_relayed(0, k, 1)
+
+    for j in range(loads):
+        swapped(j).wait_recv()
+    dps = range(days)
+    transform(0, 0, dps, first_h)
+
+    mask_copy.wait_recv()
+    for o in range(1, peers + 1):
+        told(o).wait_recv()
+    ours, other = stat_out[...], jnp.zeros_like(stat_out)
+    for o in range(1, peers + 1):
+        if o % 2:
+            other = other + stat_in[o - 1]
+        else:
+            ours = ours + stat_in[o - 1]
+    for which, stats in enumerate((ours, other)):
+        row = jnp.sum(stats, axis=1, keepdims=True)
+        power = row[:days] / (lag_count * jnp.maximum(row[days:], 1.0)) + 0.1
+        weight = lax.rsqrt(power)
+        for slot in (0, 1):
+            at = pl.multiple_of((chip ^ mine(slot)) * LANES, LANES)
+            usable = (mask_in if which else mask_ref)[:, pl.ds(at, LANES)].astype(f32)
+            by_day = weight * usable
+            offset = jnp.where(usable > 0.0, 0.25 * power, jnp.inf)
+            for d in range(days):
+                scale[slot, which * days + d] = jnp.broadcast_to(by_day[d : d + 1], (8, LANES))
+                bias[slot, which * days + d] = jnp.broadcast_to(offset[d : d + 1], (8, LANES))
+    swapped_late().wait_recv()
+
+    def step(k, carry):
+        for q in range(2):
+            transform(1, k, (q,), second_h)
+            add_days(0, k, q * HALF, HALF, first_h)
+        finish_first(k)
+        for q in range(2, 4):
+            transform(1, k, (q,), second_h)
+        ahead = jnp.minimum(k + 1, steps - 1)
+        for q in range(2):
+            transform(0, ahead, (q,), first_h)
+            add_days(1, k, q * HALF, HALF, second_h)
+        finish_second(k)
+        for q in range(2, 4):
+            transform(0, ahead, (q,), first_h)
+        return carry
+
+    lax.fori_loop(0, steps, step, 0)
+
+    def gather(k, carry):
+        for half in (0, 1):
+            @pl.when(core == 0)
+            def _():
+                handed(k, half).wait_recv()
+
+            for s in (0, 1):
+                remote(
+                    final_out.at[k, half, 0], final_in.at[s, k, half], final_send.at[k, half, 0],
+                    final_recv.at[s, k, half], partner,
+                ).wait_recv()
+                far = decode(final_in.at[s, k, half])
+                for v in range(3):
+                    total[k, half, v] += far[v]
+        return carry
+
+    lax.fori_loop(0, steps, gather, 0)
+    for k in range(steps):
+        for half in (0, 1):
+            lin, one, two = (total[k, half, v] for v in range(3))
+            for ref, value in ((linear_ref, lin), (power_ref, one * one + two * two)):
+                turned = value.T
+                for part in (0, 1):
+                    start = k * CHUNK + half * HALF + part * ROWS
+                    stop = min(start + ROWS, lag_count)
+                    if stop > start:
+                        rows = turned[part * LANES // 2 : (part + 1) * LANES // 2]
+                        ref[:, start:stop] = rows[:, : stop - start]
+
+    mask_copy.wait_send()
+    swapped_late().wait_send()
+    for j in range(loads):
+        swapped(j).wait_send()
+    for o in range(1, peers + 1):
+        told(o).wait_send()
+    for k in range(steps):
+        for half in (0, 1):
+            for c in (0, 1):
+                finished(k, half, c).wait_send()
+
+            @pl.when(core == 0)
+            def _():
+                relayed(k, half).wait_send()
+
+            @pl.when(core == 1)
+            def _():
+                handed(k, half).wait_send()
+
+
+def fast_sums(correlations, mask):
+    days, pairs, lag_count = correlations.shape
+    owned = pairs // lax.axis_size("day")
+    peers = 2 * lax.axis_size("pair") - 1
+    tiles = pairs // LANES
+    planes = tiles * days
+    width = chunked(lag_count)
+    steps, loads = width // CHUNK, width // TILE
+    by_lag = correlations.transpose(2, 0, 1).reshape(lag_count, days, tiles, LANES)
+    by_lag = by_lag.transpose(0, 2, 1, 3).reshape(lag_count, planes, LANES)
+    out = jax.ShapeDtypeStruct((owned, lag_count), jnp.float32)
+    vmem = pl.BlockSpec(memory_space=pltpu.VMEM)
+    hbm = pl.BlockSpec(memory_space=pl.ANY)
+    dma = pltpu.SemaphoreType.DMA
+    bf16, f32, i32 = jnp.bfloat16, jnp.float32, jnp.int32
+    return pl.pallas_call(
+        functools.partial(fast_kernel, lag_count),
+        in_specs=[hbm, vmem, vmem, vmem],
+        out_specs=(vmem, vmem),
+        out_shape=(out, out),
+        scratch_shapes=[
+            pltpu.VMEM((width, planes, LANES), bf16),
+            pltpu.VMEM((tiles, days // 2, width, TILE), bf16),
+            pltpu.VMEM((2, days // 2, width, TILE), bf16),
+            pltpu.VMEM((CHUNK, 2 * days * LANES), f32),
+            pltpu.VMEM((CHUNK, 2 * days * LANES), f32),
+            pltpu.VMEM((2, 3, CHUNK, LANES), f32),
+            pltpu.VMEM((2, 2 * days, 8, LANES), f32),
+            pltpu.VMEM((2, 2 * days, 8, LANES), f32),
+            pltpu.VMEM(mask.shape, i32),
+            pltpu.VMEM((2 * days, LANES), f32),
+            pltpu.VMEM((peers, 2 * days, LANES), f32),
+            pltpu.VMEM((steps, 2, 2, PACK, LANES), i32),
+            pltpu.VMEM((steps, 2, PACK, LANES), i32),
+            pltpu.VMEM((steps, 2, 2, PACK, LANES), i32),
+            pltpu.VMEM((2, steps, 2, PACK, LANES), i32),
+            pltpu.VMEM((steps, 2, 3, ROWS, LANES), f32),
+            pltpu.VMEM((steps, 2, 3, ROWS, LANES), f32),
+            dma((loads,)), dma((loads,)), dma((loads,)), dma, dma, dma, dma, dma((peers,)), dma((peers,)),
+            dma((steps, 2)), dma((steps,)), dma((steps, 2, 2)), dma((2, steps, 2)), dma((steps, 2)), dma((steps, 2)),
+        ],
+        compiler_params=pltpu.CompilerParams(
+            vmem_limit_bytes=58 * 2**20, collective_id=0, has_side_effects=True
+        ),
+        name="stack",
+    )(by_lag, mask, jnp.asarray(block_strip(lag_count)), jnp.asarray(sorting_matrix(planes)))
+
+
+def shards(correlations, mask, counts):
+    days, pairs, lag_count = correlations.shape
+    groups = lax.axis_size("day")
+    fits = groups == 8 and days == 4 and pairs == groups // 2 * LANES
+    linear_sum, power = (fast_sums if fits else general_sums)(correlations, mask)
     inverse = (1.0 / jnp.maximum(counts.astype(jnp.float32), 1.0))[:, None]
     linear = linear_sum * inverse
     return (linear * (power * (inverse * inverse)), linear)

time: 61.8 us -> 59.3 us (0.960); the launches traced: 60.7 us -> 59.2 us
  local copies, waits for them, and re-layouts: 13.9 us -> 0 us
  Pallas kernels: 45 us -> 55.6 us
  other arithmetic: 1.11 us -> 2.97 us
    unnamed x7 -> x0, local copies, waits for them, and re-layouts: 13.9 us -> none
    pallas_call x1, Pallas kernels: 45 us -> 55.6 us  [fast_sums(): pl.pallas_call(functools.partial(fast_kernel, lag_count), in_specs=[hbm,...]
    mul x2, other arithmetic: 1.11 us -> 2.97 us  [shards(): return (linear * (power * (inverse * inverse)), linear)]
where the time goes in v1:
time: 59.3 us; the launch traced here: 59.2 us
  Pallas kernels  55.6 us (94%)
  other arithmetic  2.97 us (5%)
  between operations  0.64 us (1%)
    pallas_call x1, Pallas kernels, fast_sums(): pl.pallas_call(functools.partial(fast_kernel, lag_count), in_specs=[hbm,...  55.6 us
    mul x2, other arithmetic, shards(): return (linear * (power * (inverse * inverse)), linear)  2.97 us

profile of v1, /device:TPU:1, one launch (start us, length us, event | category | flops | bytes accessed | tf_op | source)
XLA Modules:
  0.0 59.2 jit_solution(5072046408742050002)
XLA Ops:
  0.6 0.7 %fusion = (f32[64]{0:T(128)S(1)}, f32[64]{0:T(128)S(1)}) fusion(s32[64]{0:T(128)} %param.7), kind=kLoop, calls=%fused_computation.3 | loop fusion | flops 256 | bytes 768 | tf_op jit(solution)/shard_map/mul | solution.py:726
  1.3 55.6 %stack.1 = (f32[64,2001]{1,0:T(8,128)}, f32[64,2001]{1,0:T(8,128)}) custom-call(bf16[2001,16,128]{2,1,0:T(8,128)(2,1)} %bitcast.7, s32[4,512]{1,0:T(4,128)} %mask_ref.1, bf16[256,3840]{1,0:T(8,128)(2,1)} %constant.6.clone.strip, bf16[256,256]{1,0:T(8,128)(2,1)} %constant.7.clone.sorter), custom_call_target="tpu_custom_call" | custom-call | tf_op jit(solution)/shard_map/stack/pallas_call | solution.py:686
  56.9 2.3 %multiply_multiply_fusion = (f32[64,2001]{1,0:T(8,128)}, f32[64,2001]{1,0:T(8,128)}) fusion(f32[64,2001]{1,0:T(8,128)} %get-tuple-element.5, f32[64]{0:T(128)S(1)} %get-tuple-element.8, f32[64,2001]{1,0:T(8,128)} %get-tuple-element.4, f32[64]{0:T(128)S(1)} %get-tuple-element.9), kind=kLoop, calls=%fused_computation | loop fusion | flops 384192 | bytes 2049536 | tf_op jit(solution)/shard_map/mul | solution.py:726

commit v2 on v1

--- a/solution.py
+++ b/solution.py
@@ -321,6 +321,7 @@
 ROWS = HALF // 2
 WORDS = ROWS + ROWS // 2
 PACK = WORDS + 8
+SENT = WORDS + 3
 
 
 def block_strip(lag_count):
@@ -348,17 +349,18 @@
 
 
 def fast_kernel(
-    lag_count, x_hbm, mask_ref, strip, sorter, linear_ref, power_ref,
-    raw, own, theirs, first_h, second_h, sums, scale, bias, mask_in, stat_out, stat_in,
-    partial_out, partial_in, final_out, final_in, own_out, total,
-    load_sem, swap_send, swap_recv, late_send, late_recv, mask_send, mask_recv, stat_send, stat_recv,
+    lag_count, x_hbm, mask_ref, counts_ref, strip_hbm, sorter, weighted_ref, linear_ref,
+    raw, own, theirs, strip, even_h, odd_h, sums, scale, bias, mask_in, stat_out, stat_in,
+    coded, parts, partial_in, relay_out, final_in, total, inverse,
+    load_sem, strip_sem, swap_send, swap_recv, late_send, late_recv, mask_send, mask_recv, stat_send, stat_recv,
     partial_send, partial_recv, final_send, final_recv, own_send, own_recv,
 ):
     f32 = jnp.float32
     width = raw.shape[0]
     planes = raw.shape[1]
     loads = width // TILE
-    steps = width // CHUNK
+    chunks = width // CHUNK
+    steps = 2 * chunks
     peers = stat_in.shape[0]
     days = mask_ref.shape[0]
     tiles = mask_ref.shape[1] // LANES
@@ -367,6 +369,15 @@
     chip, core = me // 2, me % 2
     partner = {"day": me ^ 1, "pair": plane}
 
+    def order(s):
+        inner = (s + 1) % 2
+        slot = jnp.where(s == 0, 0, jnp.where(s == steps - 1, 1, inner))
+        k = jnp.where(s == 0, 0, jnp.where(s == steps - 1, chunks - 1, jnp.where(inner == 0, (s + 1) // 2, (s - 2) // 2)))
+        return jnp.where(core == 0, slot, s // chunks), jnp.where(core == 0, k, s % chunks)
+
+    def near_step(k):
+        return jnp.where(core == 0, jnp.where(k == chunks - 1, steps - 1, 2 * k + 2), k)
+
     def near(o, c):
         return {"day": 2 * (chip ^ o) + c, "pair": plane}
 
@@ -398,25 +409,31 @@
     def told(o):
         return remote(stat_out, stat_in.at[o - 1], stat_send.at[o - 1], stat_recv.at[o - 1], peer(o))
 
-    def relayed(k, half):
+    sent = pl.ds(0, SENT)
+
+    def relayed(s, k, half):
         return remote(
-            partial_out.at[k, half], partial_in.at[k], partial_send.at[k, half], partial_recv.at[k],
+            coded.at[s, half, :, sent], partial_in.at[k, :, sent], partial_send.at[k, half], partial_recv.at[k],
             near(1 + half, half),
         )
 
-    def finished(k, half, c):
+    def finished(source, k, half, c):
         return remote(
-            final_out.at[k, half, c], final_in.at[1 - core, k, half], final_send.at[k, half, c],
+            source.at[sent], final_in.at[1 - core, k, half, sent], final_send.at[k, half, c],
             final_recv.at[1 - core, k, half], near(2 - core, c),
         )
 
-    def handed(k, half):
-        return remote(own_out.at[k, half], total.at[k, half], own_send.at[k, half], own_recv.at[k, half], partner)
+    def handed(s, k, half):
+        return remote(
+            parts.at[s, half, 0], total.at[k, half], own_send.at[k, half], own_recv.at[k, half], partner
+        )
 
     last = loads - 1
     for j in range(last):
         loaded(j).start()
     loaded(last, lag_count - last * TILE).start()
+    strip_copy = pltpu.make_async_copy(strip_hbm, strip, strip_sem)
+    strip_copy.start()
     barrier = pltpu.get_barrier_semaphore()
     for o in range(1, peers + 1):
         pl.semaphore_signal(barrier, inc=1, device_id=peer(o), device_id_type=MESH)
@@ -478,9 +495,9 @@
                     strip[:, pl.ds(start, width)], rhs, preferred_element_type=f32
                 )
 
-    def add_days(slot, k, first, count, source):
+    def add_days(slot, k, source):
         size = 32
-        for row in range(first, first + count, size):
+        for row in range(0, CHUNK, size):
             at = pl.multiple_of(k * CHUNK + row, size)
             lin = one = two = jnp.zeros((size // 8, 8, LANES), f32)
             for e in range(2 * days):
@@ -496,26 +513,26 @@
                 one = one + x * r
                 two = two + h * r
             for v, value in enumerate((lin, one, two)):
-                sums[slot, v, row : row + size] = value.reshape(size, LANES)
+                sums[v, row : row + size] = value.reshape(size, LANES)
 
     low_lane = lax.broadcasted_iota(jnp.int32, (ROWS, LANES), 1) < LANES // 2
 
-    def split(slot, half, v, c):
-        a = sums[slot, v, half * HALF : half * HALF + ROWS]
-        b = sums[slot, v, half * HALF + ROWS : (half + 1) * HALF]
+    def split(half, v, c):
+        a = sums[v, half * HALF : half * HALF + ROWS]
+        b = sums[v, half * HALF + ROWS : (half + 1) * HALF]
         if c == 0:
             return jnp.where(low_lane, a, pltpu.roll(b, LANES // 2, 1))
         return jnp.where(low_lane, pltpu.roll(a, LANES // 2, 1), b)
 
     def encode(target, values):
-        coded, units = [], []
+        codes_of, units = [], []
         for value in values:
             top = jnp.max(jnp.abs(value), axis=0, keepdims=True)
             unit = (top * UNIT).astype(jnp.int32) + 1
             step = FULL * UNIT / unit.astype(f32)
-            coded.append((value * step + 32768.5).astype(jnp.int32))
+            codes_of.append((value * step + 32768.5).astype(jnp.int32))
             units.append(unit)
-        lin, one, two = coded
+        lin, one, two = codes_of
         target[:ROWS] = one * 65536 + two
         target[ROWS:WORDS] = lin[: ROWS // 2] * 65536 + lin[ROWS // 2 :]
         pick = lax.broadcasted_iota(jnp.int32, (8, LANES), 0)
@@ -534,49 +551,46 @@
         top, bottom = pieces(source[ROWS:WORDS])
         return (jnp.concatenate([value(top, 0), value(bottom, 0)], axis=0), value(one, 1), value(two, 2))
 
-    def send_direct(slot, k, half):
-        for c in (0, 1):
-            encode(final_out.at[k, half, c], [split(slot, half, v, c) for v in range(3)])
-            finished(k, half, c).start()
-
-    def send_relayed(slot, k, half):
-        relayed(k, half).wait_recv()
+    def reduce_days(s, source):
+        slot, k = order(s)
+        add_days(slot, k, source)
+        for half in (0, 1):
+            for c in (0, 1):
+                values = [split(half, v, c) for v in range(3)]
+                for v in range(3):
+                    parts[s, half, c, v] = values[v]
+                encode(coded.at[s, half, c], values)
+
+    def send(s):
+        slot, k = order(s)
+
+        @pl.when(slot + core == 1)
+        def _():
+            for c in (0, 1):
+                finished(coded.at[s, 1 - core, c], k, 1 - core, c).start()
+
+        @pl.when(slot + core == 0)
+        def _():
+            for half in (0, 1):
+                relayed(s, k, half).start()
+
+        @pl.when(slot + core == 2)
+        def _():
+            for half in (0, 1):
+                handed(s, k, half).start()
+
+    def relay(k):
+        relayed(0, k, 0).wait_recv()
         for c in (0, 1):
             far = decode(partial_in.at[k, c])
-            encode(final_out.at[k, half, c], [split(slot, half, v, c) + far[v] for v in range(3)])
-            finished(k, half, c).start()
-
-    def finish_first(k):
-        @pl.when(core == 0)
-        def _():
-            for half in (0, 1):
-                for c in (0, 1):
-                    encode(partial_out.at[k, half, c], [split(0, half, v, c) for v in range(3)])
-                relayed(k, half).start()
-
-        @pl.when(core == 1)
-        def _():
-            send_direct(0, k, 0)
-
-    def finish_second(k):
-        @pl.when(core == 0)
-        def _():
-            send_direct(1, k, 1)
-            send_relayed(1, k, 0)
-
-        @pl.when(core == 1)
-        def _():
-            for half in (0, 1):
-                for v in range(3):
-                    own_out[k, half, v] = split(1, half, v, 0)
-                    total[k, half, v] = split(1, half, v, 1)
-                handed(k, half).start()
-            send_relayed(0, k, 1)
+            encode(relay_out.at[k, c], [parts[near_step(k), core, c, v] + far[v] for v in range(3)])
+            finished(relay_out.at[k, c], k, core, c).start()
 
     for j in range(loads):
         swapped(j).wait_recv()
     dps = range(days)
-    transform(0, 0, dps, first_h)
+    strip_copy.wait()
+    transform(*order(0), dps, even_h)
 
     mask_copy.wait_recv()
     for o in range(1, peers + 1):
@@ -599,35 +613,45 @@
             for d in range(days):
                 scale[slot, which * days + d] = jnp.broadcast_to(by_day[d : d + 1], (8, LANES))
                 bias[slot, which * days + d] = jnp.broadcast_to(offset[d : d + 1], (8, LANES))
+    transform(*order(1), dps[:2], odd_h)
+    reduce_days(0, even_h)
+    send(0)
+    transform(*order(1), dps[2:], odd_h)
     swapped_late().wait_recv()
 
-    def step(k, carry):
-        for q in range(2):
-            transform(1, k, (q,), second_h)
-            add_days(0, k, q * HALF, HALF, first_h)
-        finish_first(k)
-        for q in range(2, 4):
-            transform(1, k, (q,), second_h)
-        ahead = jnp.minimum(k + 1, steps - 1)
-        for q in range(2):
-            transform(0, ahead, (q,), first_h)
-            add_days(1, k, q * HALF, HALF, second_h)
-        finish_second(k)
-        for q in range(2, 4):
-            transform(0, ahead, (q,), first_h)
+    def step(i, carry):
+        for s, target, source in ((2 * i + 1, even_h, odd_h), (2 * i + 2, odd_h, even_h)):
+            transform(*order(s + 1), dps, target)
+            reduce_days(s, source)
+            send(s)
+            if source is odd_h:
+                @pl.when(i >= 1)
+                def _():
+                    relay(i - 1)
         return carry
 
-    lax.fori_loop(0, steps, step, 0)
+    lax.fori_loop(0, chunks - 1, step, 0)
+    reduce_days(steps - 1, odd_h)
+    send(steps - 1)
+    lax.fori_loop(chunks - 2, chunks, lambda k, carry: (relay(k), carry)[1], 0)
+    one_over = 1.0 / jnp.maximum(counts_ref[...].astype(f32), 1.0)
+    inverse[:, : LANES // 2] = one_over
+    inverse[:, LANES // 2 :] = one_over
 
     def gather(k, carry):
         for half in (0, 1):
             @pl.when(core == 0)
             def _():
-                handed(k, half).wait_recv()
+                handed(0, k, half).wait_recv()
+
+            @pl.when(core == 1)
+            def _():
+                for v in range(3):
+                    total[k, half, v] = parts[chunks + k, half, 1, v]
 
             for s in (0, 1):
                 remote(
-                    final_out.at[k, half, 0], final_in.at[s, k, half], final_send.at[k, half, 0],
+                    relay_out.at[k, 0, sent], final_in.at[s, k, half, sent], final_send.at[k, half, 0],
                     final_recv.at[s, k, half], partner,
                 ).wait_recv()
                 far = decode(final_in.at[s, k, half])
@@ -635,11 +659,14 @@
                     total[k, half, v] += far[v]
         return carry
 
-    lax.fori_loop(0, steps, gather, 0)
-    for k in range(steps):
+    lax.fori_loop(0, chunks, gather, 0)
+    over = inverse[...]
+    for k in range(chunks):
         for half in (0, 1):
             lin, one, two = (total[k, half, v] for v in range(3))
-            for ref, value in ((linear_ref, lin), (power_ref, one * one + two * two)):
+            lin = lin * over
+            power = lin * ((one * one + two * two) * (over * over))
+            for ref, value in ((linear_ref, lin), (weighted_ref, power)):
                 turned = value.T
                 for part in (0, 1):
                     start = k * CHUNK + half * HALF + part * ROWS
@@ -654,30 +681,31 @@
         swapped(j).wait_send()
     for o in range(1, peers + 1):
         told(o).wait_send()
-    for k in range(steps):
+    for k in range(chunks):
         for half in (0, 1):
             for c in (0, 1):
-                finished(k, half, c).wait_send()
+                finished(relay_out.at[k, c], k, half, c).wait_send()
 
             @pl.when(core == 0)
             def _():
-                relayed(k, half).wait_send()
+                relayed(0, k, half).wait_send()
 
             @pl.when(core == 1)
             def _():
-                handed(k, half).wait_send()
-
-
-def fast_sums(correlations, mask):
+                handed(0, k, half).wait_send()
+
+
+def fast_stack(correlations, mask, counts):
     days, pairs, lag_count = correlations.shape
     owned = pairs // lax.axis_size("day")
     peers = 2 * lax.axis_size("pair") - 1
     tiles = pairs // LANES
     planes = tiles * days
     width = chunked(lag_count)
-    steps, loads = width // CHUNK, width // TILE
+    chunks, loads = width // CHUNK, width // TILE
     by_lag = correlations.transpose(2, 0, 1).reshape(lag_count, days, tiles, LANES)
     by_lag = by_lag.transpose(0, 2, 1, 3).reshape(lag_count, planes, LANES)
+    strip = jnp.asarray(block_strip(lag_count))
     out = jax.ShapeDtypeStruct((owned, lag_count), jnp.float32)
     vmem = pl.BlockSpec(memory_space=pltpu.VMEM)
     hbm = pl.BlockSpec(memory_space=pl.ANY)
@@ -685,42 +713,46 @@
     bf16, f32, i32 = jnp.bfloat16, jnp.float32, jnp.int32
     return pl.pallas_call(
         functools.partial(fast_kernel, lag_count),
-        in_specs=[hbm, vmem, vmem, vmem],
+        in_specs=[hbm, vmem, vmem, hbm, vmem],
         out_specs=(vmem, vmem),
         out_shape=(out, out),
         scratch_shapes=[
             pltpu.VMEM((width, planes, LANES), bf16),
             pltpu.VMEM((tiles, days // 2, width, TILE), bf16),
             pltpu.VMEM((2, days // 2, width, TILE), bf16),
+            pltpu.VMEM(strip.shape, bf16),
             pltpu.VMEM((CHUNK, 2 * days * LANES), f32),
             pltpu.VMEM((CHUNK, 2 * days * LANES), f32),
-            pltpu.VMEM((2, 3, CHUNK, LANES), f32),
+            pltpu.VMEM((3, CHUNK, LANES), f32),
             pltpu.VMEM((2, 2 * days, 8, LANES), f32),
             pltpu.VMEM((2, 2 * days, 8, LANES), f32),
             pltpu.VMEM(mask.shape, i32),
             pltpu.VMEM((2 * days, LANES), f32),
             pltpu.VMEM((peers, 2 * days, LANES), f32),
-            pltpu.VMEM((steps, 2, 2, PACK, LANES), i32),
-            pltpu.VMEM((steps, 2, PACK, LANES), i32),
-            pltpu.VMEM((steps, 2, 2, PACK, LANES), i32),
-            pltpu.VMEM((2, steps, 2, PACK, LANES), i32),
-            pltpu.VMEM((steps, 2, 3, ROWS, LANES), f32),
-            pltpu.VMEM((steps, 2, 3, ROWS, LANES), f32),
-            dma((loads,)), dma((loads,)), dma((loads,)), dma, dma, dma, dma, dma((peers,)), dma((peers,)),
-            dma((steps, 2)), dma((steps,)), dma((steps, 2, 2)), dma((2, steps, 2)), dma((steps, 2)), dma((steps, 2)),
+            pltpu.VMEM((2 * chunks, 2, 2, PACK, LANES), i32),
+            pltpu.VMEM((2 * chunks, 2, 2, 3, ROWS, LANES), f32),
+            pltpu.VMEM((chunks, 2, PACK, LANES), i32),
+            pltpu.VMEM((chunks, 2, PACK, LANES), i32),
+            pltpu.VMEM((2, chunks, 2, PACK, LANES), i32),
+            pltpu.VMEM((chunks, 2, 3, ROWS, LANES), f32),
+            pltpu.VMEM((1, LANES), f32),
+            dma((loads,)), dma, dma((loads,)), dma((loads,)), dma, dma, dma, dma, dma((peers,)), dma((peers,)),
+            dma((chunks, 2)), dma((chunks,)), dma((chunks, 2, 2)), dma((2, chunks, 2)),
+            dma((chunks, 2)), dma((chunks, 2)),
         ],
         compiler_params=pltpu.CompilerParams(
-            vmem_limit_bytes=58 * 2**20, collective_id=0, has_side_effects=True
+            vmem_limit_bytes=125 * 2**19, collective_id=0, has_side_effects=True
         ),
         name="stack",
-    )(by_lag, mask, jnp.asarray(block_strip(lag_count)), jnp.asarray(sorting_matrix(planes)))
+    )(by_lag, mask, counts.reshape(1, owned), strip, jnp.asarray(sorting_matrix(planes)))
 
 
 def shards(correlations, mask, counts):
     days, pairs, lag_count = correlations.shape
     groups = lax.axis_size("day")
-    fits = groups == 8 and days == 4 and pairs == groups // 2 * LANES
-    linear_sum, power = (fast_sums if fits else general_sums)(correlations, mask)
+    if groups == 8 and days == 4 and pairs == groups // 2 * LANES:
+        return fast_stack(correlations, mask, counts)
+    linear_sum, power = general_sums(correlations, mask)
     inverse = (1.0 / jnp.maximum(counts.astype(jnp.float32), 1.0))[:, None]
     linear = linear_sum * inverse
     return (linear * (power * (inverse * inverse)), linear)

time: 59.3 us -> 55.4 us (0.934)
  Pallas kernels: 55.6 us -> 50.7 us
  local copies, waits for them, and re-layouts: 0 us -> 3.74 us
  other arithmetic: 2.97 us -> 0 us
    pallas_call x1, Pallas kernels: 55.6 us -> 50.7 us  [fast_stack(): pl.pallas_call(functools.partial(fast_kernel, lag_count), in_specs=[hbm,...]
    unnamed x0 -> x2, local copies, waits for them, and re-layouts: none -> 3.74 us
    mul x2 -> x0, other arithmetic: 2.97 us -> none  [shards(): return (linear * (power * (inverse * inverse)), linear)]
where the time goes in v2:
time: 55.4 us; the launch traced here: 55.1 us
  Pallas kernels  50.7 us (92%)
  local copies, waits for them, and re-layouts  3.74 us (7%)
  between operations  0.64 us (1%)
    pallas_call x1, Pallas kernels, fast_stack(): pl.pallas_call(functools.partial(fast_kernel, lag_count), in_specs=[hbm,...  50.7 us
    unnamed x2, local copies, waits for them, and re-layouts  3.74 us

profile of v2, /device:TPU:1, one launch (start us, length us, event | category | flops | bytes accessed | tf_op | source)
XLA Modules:
  0.0 55.1 jit_solution(11815134088096509250)
XLA Ops:
  0.6 50.7 %stack.1 = (f32[64,2001]{1,0:T(8,128)}, f32[64,2001]{1,0:T(8,128)}) custom-call(bf16[2001,16,128]{2,1,0:T(8,128)(2,1)} %bitcast.8, s32[4,512]{1,0:T(4,128)} %mask_ref.1, s32[1,64]{1,0:T(1,128)} %bitcast.9, bf16[256,3840]{1,0:T(8,128)(2,1)} %constant.4.clone.strip_hbm, bf16[256,256]{1,0:T(8,128)(2,1)} %constant.5.clone.sorter), custom_call_target="tpu_custom_call" | custom-call | tf_op jit(solution)/shard_map/stack/pallas_call | solution.py:714
  51.4 1.9 %copy.10 = f32[64,2001]{1,0:T(8,128)} copy(f32[64,2001]{1,0:T(8,128)} %get-tuple-element.4) | data formatting | bytes 1024512
  53.3 1.9 %copy.11 = f32[64,2001]{1,0:T(8,128)} copy(f32[64,2001]{1,0:T(8,128)} %get-tuple-element.5) | data formatting | bytes 1024512

commit v3 on v2

--- a/solution.py
+++ b/solution.py
@@ -349,10 +349,10 @@
 
 
 def fast_kernel(
-    lag_count, x_hbm, mask_ref, counts_ref, strip_hbm, sorter, weighted_ref, linear_ref,
-    raw, own, theirs, strip, even_h, odd_h, sums, scale, bias, mask_in, stat_out, stat_in,
-    coded, parts, partial_in, relay_out, final_in, total, inverse,
-    load_sem, strip_sem, swap_send, swap_recv, late_send, late_recv, mask_send, mask_recv, stat_send, stat_recv,
+    lag_count, x_hbm, mask_hbm, counts_hbm, strip_hbm, sorter_hbm, power_ref, linear_ref, inverse_ref,
+    mask_ref, counts_ref, sorter, raw, own, theirs, strip, even_h, odd_h, sums, scale, bias, mask_in, stat_out, stat_in,
+    coded, parts, partial_in, relay_out, final_in, total,
+    load_sem, small_sem, swap_send, swap_recv, late_send, late_recv, mask_send, mask_recv, stat_send, stat_recv,
     partial_send, partial_recv, final_send, final_recv, own_send, own_recv,
 ):
     f32 = jnp.float32
@@ -369,14 +369,14 @@
     chip, core = me // 2, me % 2
     partner = {"day": me ^ 1, "pair": plane}
 
+    def pick(s, table):
+        return sum(jnp.where(s == i, value, 0) for i, value in enumerate(table))
+
     def order(s):
-        inner = (s + 1) % 2
-        slot = jnp.where(s == 0, 0, jnp.where(s == steps - 1, 1, inner))
-        k = jnp.where(s == 0, 0, jnp.where(s == steps - 1, chunks - 1, jnp.where(inner == 0, (s + 1) // 2, (s - 2) // 2)))
-        return jnp.where(core == 0, slot, s // chunks), jnp.where(core == 0, k, s % chunks)
-
-    def near_step(k):
-        return jnp.where(core == 0, jnp.where(k == chunks - 1, steps - 1, 2 * k + 2), k)
+        return (
+            jnp.where(core == 0, pick(s, (0, 0, 0, 1, 0, 1, 1, 1)), s // chunks),
+            jnp.where(core == 0, pick(s, (0, 2, 1, 0, 3, 1, 2, 3)), pick(s, (2, 3, 0, 1, 0, 1, 2, 3))),
+        )
 
     def near(o, c):
         return {"day": 2 * (chip ^ o) + c, "pair": plane}
@@ -412,9 +412,10 @@
     sent = pl.ds(0, SENT)
 
     def relayed(s, k, half):
+        far = k // 2
         return remote(
-            coded.at[s, half, :, sent], partial_in.at[k, :, sent], partial_send.at[k, half], partial_recv.at[k],
-            near(1 + half, half),
+            coded.at[s, half, :, sent], partial_in.at[k % 2, half, :, sent], partial_send.at[k, half],
+            partial_recv.at[k % 2, half], near(2 - far, 1 - far),
         )
 
     def finished(source, k, half, c):
@@ -429,11 +430,18 @@
         )
 
     last = loads - 1
+    small = [
+        pltpu.make_async_copy(source, target, small_sem.at[i])
+        for i, (source, target) in enumerate(
+            ((sorter_hbm, sorter), (mask_hbm, mask_ref), (counts_hbm, counts_ref), (strip_hbm, strip))
+        )
+    ]
+    for copy in small[:3]:
+        copy.start()
     for j in range(last):
         loaded(j).start()
     loaded(last, lag_count - last * TILE).start()
-    strip_copy = pltpu.make_async_copy(strip_hbm, strip, strip_sem)
-    strip_copy.start()
+    small[3].start()
     barrier = pltpu.get_barrier_semaphore()
     for o in range(1, peers + 1):
         pl.semaphore_signal(barrier, inc=1, device_id=peer(o), device_id_type=MESH)
@@ -442,6 +450,8 @@
             pl.semaphore_signal(barrier, inc=1, device_id=near(o, c), device_id_type=MESH)
     raw[lag_count:] = jnp.zeros((width - lag_count, planes, LANES), raw.dtype)
     pl.semaphore_wait(barrier, peers + 4)
+    small[0].wait()
+    small[1].wait()
     mask_copy = remote(mask_ref, mask_in, mask_send, mask_recv, partner)
     mask_copy.start()
 
@@ -486,18 +496,22 @@
     def operand(slot, dp):
         return own[mine(slot), dp] if dp < days // 2 else theirs[slot, dp - days // 2]
 
-    def transform(slot, k, dps, target):
-        for dp in dps:
-            rhs = operand(slot, dp)
-            for part in range(CHUNK // TILE):
-                start = pl.multiple_of(width - TILE - (k * (CHUNK // TILE) + part) * TILE, TILE)
-                target[part * TILE : (part + 1) * TILE, dp * TILE : (dp + 1) * TILE] = jnp.dot(
-                    strip[:, pl.ds(start, width)], rhs, preferred_element_type=f32
-                )
-
-    def add_days(slot, k, source):
+    parts_of = CHUNK // TILE
+
+    def transform_piece(slot, k, piece, target):
+        dp, part = piece // parts_of, piece % parts_of
+        start = pl.multiple_of(width - TILE - (k * parts_of + part) * TILE, TILE)
+        target[part * TILE : (part + 1) * TILE, dp * TILE : (dp + 1) * TILE] = jnp.dot(
+            strip[:, pl.ds(start, width)], operand(slot, dp), preferred_element_type=f32
+        )
+
+    def transform(slot, k, pieces, target):
+        for piece in pieces:
+            transform_piece(slot, k, piece, target)
+
+    def add_days(slot, k, first, stop, source):
         size = 32
-        for row in range(0, CHUNK, size):
+        for row in range(first, stop, size):
             at = pl.multiple_of(k * CHUNK + row, size)
             lin = one = two = jnp.zeros((size // 8, 8, LANES), f32)
             for e in range(2 * days):
@@ -551,46 +565,62 @@
         top, bottom = pieces(source[ROWS:WORDS])
         return (jnp.concatenate([value(top, 0), value(bottom, 0)], axis=0), value(one, 1), value(two, 2))
 
-    def reduce_days(s, source):
+    def code(s, half, c):
+        values = [split(half, v, c) for v in range(3)]
+        for v in range(3):
+            parts[s, half, c, v] = values[v]
+        encode(coded.at[s, half, c], values)
+
+    def step_both(s, source, target):
         slot, k = order(s)
-        add_days(slot, k, source)
-        for half in (0, 1):
-            for c in (0, 1):
-                values = [split(half, v, c) for v in range(3)]
-                for v in range(3):
-                    parts[s, half, c, v] = values[v]
-                encode(coded.at[s, half, c], values)
-
-    def send(s):
+        rows = (0, 96, 192, 288, 384, 448, CHUNK)
+        for piece in range(2 * days):
+            if piece < len(rows) - 1:
+                add_days(slot, k, rows[piece], rows[piece + 1], source)
+            if piece in (3, 4):
+                code(s, 0, piece - 3)
+            if piece in (6, 7):
+                code(s, 1, piece - 6)
+            if target is not None:
+                transform_piece(*order(s + 1), piece, target)
+
+    def send(s, halves=(0, 1)):
         slot, k = order(s)
 
-        @pl.when(slot + core == 1)
+        @pl.when(jnp.logical_and(slot + core == 1, k // 2 == core))
         def _():
-            for c in (0, 1):
-                finished(coded.at[s, 1 - core, c], k, 1 - core, c).start()
+            for half in halves:
+                for c in (0, 1):
+                    finished(coded.at[s, half, c], k, half, c).start()
 
         @pl.when(slot + core == 0)
         def _():
-            for half in (0, 1):
+            for half in halves:
                 relayed(s, k, half).start()
 
         @pl.when(slot + core == 2)
         def _():
-            for half in (0, 1):
+            for half in halves:
                 handed(s, k, half).start()
 
-    def relay(k):
-        relayed(0, k, 0).wait_recv()
-        for c in (0, 1):
-            far = decode(partial_in.at[k, c])
-            encode(relay_out.at[k, c], [parts[near_step(k), core, c, v] + far[v] for v in range(3)])
-            finished(relay_out.at[k, c], k, core, c).start()
+    def relay(r):
+        k = r + 2 * (1 - core)
+        s = r + jnp.where(core == 0, steps - 2, 2)
+        def one(half, carry):
+            relayed(0, r, half).wait_recv()
+            for c in (0, 1):
+                far = decode(partial_in.at[r, half, c])
+                encode(relay_out.at[r, half, c], [parts[s, half, c, v] + far[v] for v in range(3)])
+                finished(relay_out.at[r, half, c], k, half, c).start()
+            return carry
+
+        lax.fori_loop(0, 2, one, 0)
 
     for j in range(loads):
         swapped(j).wait_recv()
-    dps = range(days)
-    strip_copy.wait()
-    transform(*order(0), dps, even_h)
+    small[3].wait()
+    transform(*order(0), range(2 * days), even_h)
+    transform(*order(1), range(days), odd_h)
 
     mask_copy.wait_recv()
     for o in range(1, peers + 1):
@@ -613,60 +643,96 @@
             for d in range(days):
                 scale[slot, which * days + d] = jnp.broadcast_to(by_day[d : d + 1], (8, LANES))
                 bias[slot, which * days + d] = jnp.broadcast_to(offset[d : d + 1], (8, LANES))
-    transform(*order(1), dps[:2], odd_h)
-    reduce_days(0, even_h)
-    send(0)
-    transform(*order(1), dps[2:], odd_h)
+    for half in (0, 1):
+        for i in range(2):
+            first = half * HALF + i * ROWS
+            add_days(*order(0), first, first + ROWS, even_h)
+            if i:
+                code(0, half, 0)
+                code(0, half, 1)
+            transform_piece(*order(1), days + 2 * half + i, odd_h)
+        send(0, (half,))
     swapped_late().wait_recv()
 
     def step(i, carry):
         for s, target, source in ((2 * i + 1, even_h, odd_h), (2 * i + 2, odd_h, even_h)):
-            transform(*order(s + 1), dps, target)
-            reduce_days(s, source)
+            step_both(s, source, target)
             send(s)
             if source is odd_h:
-                @pl.when(i >= 1)
+                @pl.when(jnp.logical_and(core == 1, i >= 1))
                 def _():
                     relay(i - 1)
+            else:
+                @pl.when(jnp.logical_and(core == 0, i == chunks - 2))
+                def _():
+                    relay(0)
         return carry
 
     lax.fori_loop(0, chunks - 1, step, 0)
-    reduce_days(steps - 1, odd_h)
+    step_both(steps - 1, odd_h, None)
     send(steps - 1)
-    lax.fori_loop(chunks - 2, chunks, lambda k, carry: (relay(k), carry)[1], 0)
-    one_over = 1.0 / jnp.maximum(counts_ref[...].astype(f32), 1.0)
-    inverse[:, : LANES // 2] = one_over
-    inverse[:, LANES // 2 :] = one_over
-
-    def gather(k, carry):
-        for half in (0, 1):
+
+    @pl.when(core == 0)
+    def _():
+        relay(1)
+
+    small[2].wait()
+    inverse_ref[...] = 1.0 / jnp.maximum(counts_ref[...].astype(f32), 1.0)
+
+    @pl.when(core == 0)
+    def _():
+        for k in range(chunks):
+            for half in (0, 1):
+                handed(0, k, half).wait_recv()
+
+    @pl.when(core == 1)
+    def _():
+        def keep(k, carry):
+            for half in (0, 1):
+                for v in range(3):
+                    total[k, half, v] = parts[chunks + k, half, 1, v]
+            return carry
+
+        lax.fori_loop(0, chunks, keep, 0)
+
+    def settle():
+        mask_copy.wait_send()
+        swapped_late().wait_send()
+        for j in range(loads):
+            swapped(j).wait_send()
+        for o in range(1, peers + 1):
+            told(o).wait_send()
+        for k in range(chunks):
+            for half in (0, 1):
+                for c in (0, 1):
+                    finished(relay_out.at[0, 0, 0], k, half, c).wait_send()
+
             @pl.when(core == 0)
             def _():
-                handed(0, k, half).wait_recv()
+                for half in (0, 1):
+                    relayed(0, k, half).wait_send()
 
             @pl.when(core == 1)
             def _():
+                for half in (0, 1):
+                    handed(0, k, half).wait_send()
+
+    seen = set()
+    for s, k in ((0, 2), (1, 0), (0, 3), (1, 1), (0, 0), (1, 2), (0, 1), (1, 3)):
+        if (s, k) == (1, 3):
+            settle()
+        for half in (0, 1):
+            remote(
+                relay_out.at[0, 0, 0, sent], final_in.at[s, k, half, sent], final_send.at[k, half, 0],
+                final_recv.at[s, k, half], partner,
+            ).wait_recv()
+            found = decode(final_in.at[s, k, half])
+            if k not in seen:
                 for v in range(3):
-                    total[k, half, v] = parts[chunks + k, half, 1, v]
-
-            for s in (0, 1):
-                remote(
-                    relay_out.at[k, 0, sent], final_in.at[s, k, half, sent], final_send.at[k, half, 0],
-                    final_recv.at[s, k, half], partner,
-                ).wait_recv()
-                far = decode(final_in.at[s, k, half])
-                for v in range(3):
-                    total[k, half, v] += far[v]
-        return carry
-
-    lax.fori_loop(0, chunks, gather, 0)
-    over = inverse[...]
-    for k in range(chunks):
-        for half in (0, 1):
-            lin, one, two = (total[k, half, v] for v in range(3))
-            lin = lin * over
-            power = lin * ((one * one + two * two) * (over * over))
-            for ref, value in ((linear_ref, lin), (weighted_ref, power)):
+                    total[k, half, v] += found[v]
+                continue
+            lin, one, two = (total[k, half, v] + found[v] for v in range(3))
+            for ref, value in ((linear_ref, lin), (power_ref, one * one + two * two)):
                 turned = value.T
                 for part in (0, 1):
                     start = k * CHUNK + half * HALF + part * ROWS
@@ -674,25 +740,7 @@
                     if stop > start:
                         rows = turned[part * LANES // 2 : (part + 1) * LANES // 2]
                         ref[:, start:stop] = rows[:, : stop - start]
-
-    mask_copy.wait_send()
-    swapped_late().wait_send()
-    for j in range(loads):
-        swapped(j).wait_send()
-    for o in range(1, peers + 1):
-        told(o).wait_send()
-    for k in range(chunks):
-        for half in (0, 1):
-            for c in (0, 1):
-                finished(relay_out.at[k, c], k, half, c).wait_send()
-
-            @pl.when(core == 0)
-            def _():
-                relayed(0, k, half).wait_send()
-
-            @pl.when(core == 1)
-            def _():
-                handed(0, k, half).wait_send()
+        seen.add(k)
 
 
 def fast_stack(correlations, mask, counts):
@@ -706,17 +754,21 @@
     by_lag = correlations.transpose(2, 0, 1).reshape(lag_count, days, tiles, LANES)
     by_lag = by_lag.transpose(0, 2, 1, 3).reshape(lag_count, planes, LANES)
     strip = jnp.asarray(block_strip(lag_count))
+    sorter = jnp.asarray(sorting_matrix(planes))
     out = jax.ShapeDtypeStruct((owned, lag_count), jnp.float32)
     vmem = pl.BlockSpec(memory_space=pltpu.VMEM)
-    hbm = pl.BlockSpec(memory_space=pl.ANY)
+    hbm = pl.BlockSpec(memory_space=pltpu.HBM)
     dma = pltpu.SemaphoreType.DMA
     bf16, f32, i32 = jnp.bfloat16, jnp.float32, jnp.int32
-    return pl.pallas_call(
+    power, linear_sum, inverse = pl.pallas_call(
         functools.partial(fast_kernel, lag_count),
-        in_specs=[hbm, vmem, vmem, hbm, vmem],
-        out_specs=(vmem, vmem),
-        out_shape=(out, out),
+        in_specs=[hbm] * 5,
+        out_specs=(vmem, vmem, vmem),
+        out_shape=(out, out, jax.ShapeDtypeStruct((1, owned), f32)),
         scratch_shapes=[
+            pltpu.VMEM(mask.shape, i32),
+            pltpu.VMEM((1, owned), i32),
+            pltpu.VMEM(sorter.shape, bf16),
             pltpu.VMEM((width, planes, LANES), bf16),
             pltpu.VMEM((tiles, days // 2, width, TILE), bf16),
             pltpu.VMEM((2, days // 2, width, TILE), bf16),
@@ -731,29 +783,31 @@
             pltpu.VMEM((peers, 2 * days, LANES), f32),
             pltpu.VMEM((2 * chunks, 2, 2, PACK, LANES), i32),
             pltpu.VMEM((2 * chunks, 2, 2, 3, ROWS, LANES), f32),
-            pltpu.VMEM((chunks, 2, PACK, LANES), i32),
-            pltpu.VMEM((chunks, 2, PACK, LANES), i32),
+            pltpu.VMEM((2, 2, 2, PACK, LANES), i32),
+            pltpu.VMEM((2, 2, 2, PACK, LANES), i32),
             pltpu.VMEM((2, chunks, 2, PACK, LANES), i32),
             pltpu.VMEM((chunks, 2, 3, ROWS, LANES), f32),
-            pltpu.VMEM((1, LANES), f32),
-            dma((loads,)), dma, dma((loads,)), dma((loads,)), dma, dma, dma, dma, dma((peers,)), dma((peers,)),
-            dma((chunks, 2)), dma((chunks,)), dma((chunks, 2, 2)), dma((2, chunks, 2)),
+            dma((loads,)), dma((4,)), dma((loads,)), dma((loads,)), dma, dma, dma, dma, dma((peers,)), dma((peers,)),
+            dma((chunks, 2)), dma((2, 2)), dma((chunks, 2, 2)), dma((2, chunks, 2)),
             dma((chunks, 2)), dma((chunks, 2)),
         ],
         compiler_params=pltpu.CompilerParams(
-            vmem_limit_bytes=125 * 2**19, collective_id=0, has_side_effects=True
+            vmem_limit_bytes=46 * 2**20, collective_id=0, has_side_effects=True
         ),
         name="stack",
-    )(by_lag, mask, counts.reshape(1, owned), strip, jnp.asarray(sorting_matrix(planes)))
+    )(*(pltpu.with_memory_space_constraint(v, pltpu.HBM) for v in (by_lag, mask, counts.reshape(1, owned), strip, sorter)))
+    return linear_sum, power, inverse.reshape(owned, 1)
 
 
 def shards(correlations, mask, counts):
     days, pairs, lag_count = correlations.shape
     groups = lax.axis_size("day")
-    if groups == 8 and days == 4 and pairs == groups // 2 * LANES:
-        return fast_stack(correlations, mask, counts)
-    linear_sum, power = general_sums(correlations, mask)
-    inverse = (1.0 / jnp.maximum(counts.astype(jnp.float32), 1.0))[:, None]
+    four = groups == 8 and days == 4 and chunked(lag_count) == 4 * CHUNK
+    if four and pairs == 4 * LANES:
+        linear_sum, power, inverse = fast_stack(correlations, mask, counts)
+    else:
+        linear_sum, power = general_sums(correlations, mask)
+        inverse = (1.0 / jnp.maximum(counts.astype(jnp.float32), 1.0))[:, None]
     linear = linear_sum * inverse
     return (linear * (power * (inverse * inverse)), linear)
 

time: 55.4 us -> 49.8 us (0.90)
  local copies, waits for them, and re-layouts: 3.74 us -> 0 us
  Pallas kernels: 50.7 us -> 47.9 us
  other arithmetic: 0 us -> 1.11 us
    unnamed x2 -> x0, local copies, waits for them, and re-layouts: 3.74 us -> none
    pallas_call x1, Pallas kernels: 50.7 us -> 47.9 us  [fast_stack(): pl.pallas_call(functools.partial(fast_kernel, lag_count), in_specs=[hbm]...]
    mul x0 -> x2, other arithmetic: none -> 1.11 us  [shards(): return (linear * (power * (inverse * inverse)), linear)]
where the time goes in v3:
time: 49.8 us; the launch traced here: 49.7 us
  Pallas kernels  47.9 us (96%)
  other arithmetic  1.11 us (2%)
  between operations  0.65 us (1%)
    pallas_call x1, Pallas kernels, fast_stack(): pl.pallas_call(functools.partial(fast_kernel, lag_count), in_specs=[hbm]...  47.9 us
    mul x2, other arithmetic, shards(): return (linear * (power * (inverse * inverse)), linear)  1.11 us

profile of v3, /device:TPU:1, one launch (start us, length us, event | category | flops | bytes accessed | tf_op | source)
XLA Modules:
  0.0 49.7 jit_solution(13035516728397967572)
XLA Ops:
  0.6 47.9 %stack.1 = (f32[64,2001]{1,0:T(8,128)S(1)}, f32[64,2001]{1,0:T(8,128)S(1)}, f32[1,64]{1,0:T(1,128)S(1)}) custom-call(bf16[2001,16,128]{2,1,0:T(8,128)(2,1)} %bitcast.11, s32[4,512]{1,0:T(4,128)} %mask_hbm.1, s32[1,64]{1,0:T(1,128)} %bitcast.12, bf16[256,3840]{1,0:T(8,128)(2,1)} %constant.4.clone.strip_hbm, bf16[256,256]{1,0:T(8,128)(2,1)} %constant.5.clone.sorter_hbm), custom_call_target="tpu_custom_call" | custom-call | tf_op jit(solution)/shard_map/stack/pallas_call | solution.py:763
  48.5 1.1 %multiply_multiply_fusion = (f32[64,2001]{1,0:T(8,128)}, f32[64,2001]{1,0:T(8,128)}) fusion(f32[64,2001]{1,0:T(8,128)S(1)} %get-tuple-element.7, f32[64]{0:T(128)S(1)} %bitcast_multiply_fusion, f32[64,2001]{1,0:T(8,128)S(1)} %get-tuple-element.5, f32[64]{0:T(128)S(1)} %bitcast.10), kind=kLoop, calls=%fused_computation | loop fusion | flops 384192 | bytes 2049536 | tf_op jit(solution)/shard_map/mul | solution.py:812
  (1 shorter events, 0.0 us)
